TPU v7x, 1024 devices: a whole 4x8x16 slice. The times are simulated.
1024 devices in a mesh: fsdp: 64 (over x, y, core), tp: 16 (over z).
Axes of the slice: x: 4, y: 8, z: 16, core: 2. Of those that a mesh axis runs over, the one named last changes fastest.
Arguments:
- features: bfloat16 [8192, 8192], P('fsdp'), may hold values from -17 to 17
- key_partials: bfloat16 [8192, 16, 128], P('fsdp', 'tp'), may hold values from -0.109375 to 0.109375
- momentum: float32 [4096, 16, 128], P('fsdp', 'tp'), may hold values from -6 to 6
Outputs:
- update: float32 [4096, 16, 128], P('fsdp', 'tp')
- new_momentum: float32 [4096, 16, 128], P('fsdp', 'tp')
All inputs are finite; a program needn't handle non-finite values.
Results may differ from a plain program's by a relative error of at most 0.0003.
Values may be sent and summed in bfloat16 or wider, within the bound.
A program may use at most 32 MiB of HBM per device.

v0:
```python
import math

import jax
import jax.numpy as jnp
from jax import lax
from jax.sharding import PartitionSpec as P

D_W = 8192
ITERS = 5


retain = 0.95
first_coef = 3.4445
second_coef = -4.775
third_coef = 2.0315
epsilon = 1e-07
shrink = 0.2


def swapped(block, axis, distance):
    count = lax.axis_size(axis)
    route = []
    for low in range(count):
        high = low | 1 << distance
        if high != low and high < count:
            route += [(low, high), (high, low)]
    return lax.ppermute(block, axis, route)


def in_blocks(shard, dim, count):
    before, after = (shard.shape[:dim], shard.shape[dim + 1 :])
    return jnp.moveaxis(shard.reshape(*before, count, -1, *after), dim, 0)


def sent_and_summed(shard, axis, dim):
    count = lax.axis_size(axis)
    blocks = lax.all_to_all(in_blocks(shard, dim, count), axis, 0, 0, tiled=True)
    return jnp.sum(blocks, axis=0)


def gathered_total(shard, axis):
    blocks = lax.all_gather(shard, axis)
    return blocks.sum(axis=0)


def on_device(features, key_partials, momentum):
    precise = lax.Precision.HIGHEST
    contract = (((0,), (0,)), ((), ()))
    parity = lax.axis_index("tp") % 2
    own_part = key_partials[:, 0, :]
    tok_rows, width = features.shape
    head_size = key_partials.shape[2]
    rows_half = momentum.shape[0]
    blocks_count = width // (2 * rows_half)
    partner = swapped(own_part, "tp", 0)
    joined = jnp.concatenate([own_part, partner], axis=1)
    blocks = features.reshape(tok_rows, blocks_count, 2, rows_half)
    chosen = lax.dynamic_slice(
        blocks,
        (0, jnp.int32(0) // rows_half, parity, 0),
        (tok_rows, rows_half * lax.axis_size("fsdp") // rows_half, 1, rows_half),
    )
    chosen = chosen.reshape(tok_rows, rows_half * lax.axis_size("fsdp"))
    product = lax.dot_general(chosen, joined, contract, preferred_element_type=jnp.float32)
    grads = sent_and_summed(product[:, :head_size] + product[:, head_size:], "fsdp", 0)
    moment = momentum[:, 0, :]
    fresh = retain * moment + grads
    blend = grads + retain * fresh
    gram = lax.dot_general(blend, blend, contract, precision=precise)
    gram = gathered_total(gram, "fsdp")
    gram = gram + swapped(gram, "tp", 0)
    inverse = 1.0 / (jnp.sqrt(jnp.trace(gram)) + epsilon)
    state = blend * inverse
    gram = gram * (inverse * inverse)
    identity = jnp.eye(head_size, dtype=jnp.float32)
    for step in range(ITERS):
        square = jnp.dot(gram, gram, precision=precise)
        poly = first_coef * identity + second_coef * gram + third_coef * square
        state = jnp.dot(state, poly, precision=precise)
        gram = jnp.dot(poly, jnp.dot(gram, poly, precision=precise), precision=precise)
    update = shrink * math.sqrt(D_W) * state
    return (update[:, None, :], fresh[:, None, :])


def solution(mesh):
    placed = (P("fsdp", None), P("fsdp", "tp", None), P("fsdp", "tp", None))
    return jax.shard_map(
        on_device,
        mesh=mesh,
        in_specs=placed,
        out_specs=(P("fsdp", "tp", None), P("fsdp", "tp", None)),
        check_vma=False,
    )
```

profile of v0, /device:TPU:1, one launch (start us, length us, event | category | flops | bytes accessed | tf_op | source)
XLA Modules:
  0.0 200.0 jit_solution(12275215687521739561)
XLA Ops:
  7.2 4.8 %collective-permute-start = (bf16[128,128]{1,0:T(8,128)(2,1)}, bf16[128,128]{1,0:T(8,128)(2,1)S(1)}, u32[]{:S(2)}, u32[]{:S(2)}) collective-permute-start(bf16[128,128]{1,0:T(8,128)(2,1)} %bitcast.71), channel_id=1, source_target_pairs={{0,1},{1,0},{2,3},{3,2},{4,5},{5,4},{6,7},{7,6},{8,9},{9,8},{10,11... | collective-permute-start | bytes 98312 | tf_op jit(solution)/shard_map/ppermute | solution.py:27
  12.0 3.2 %copy.9 = bf16[128,8192]{0,1:T(8,128)(2,1)S(1)} copy(bf16[128,8192]{1,0:T(8,128)(2,1)} %param.3) | data formatting | bytes 4194304 | tf_op args[0]
  15.2 0.0 copy-start.1
  15.3 0.1 constant_dynamic-slice_fusion
  15.4 0.0 collective-permute-done
  15.4 0.6 copy-done.1
  16.0 0.7 fusion.5
  16.7 1.5 slice_add_fusion
  18.2 0.0 copy-start
  18.2 15.6 %all-to-all-start = ((f32[64,64,128]{2,1,0:T(8,128)}), f32[64,64,128]{2,1,0:T(8,128)S(1)}, u32[]{:S(2)}, u32[]{:S(2)}) async-start(f32[64,64,128]{2,1,0:T(8,128)} %bitcast.3), calls=%async_computation | async-start | bytes 4194304 | tf_op jit(solution)/shard_map/all_to_all | solution.py:37
  33.8 0.0 all-gather.3.cloned.1.call-start
  33.8 0.0 copy-done
  33.9 51.2 %all-to-all-done = f32[64,64,128]{2,1,0:T(8,128)S(1)} async-done(((f32[64,64,128]{2,1,0:T(8,128)}), f32[64,64,128]{2,1,0:T(8,128)S(1)}, u32[]{:S(2)}, u32[]{:S(2)}) %all-to-all-start) | async-done | bytes 2097184 | tf_op jit(solution)/shard_map/all_to_all | solution.py:37
  85.1 0.1 reduce_sum.30
  85.3 0.6 multiply_add_fusion
  85.9 0.9 fusion.25
  86.8 0.0 all-gather.3.cloned.1.call-update
  86.8 93.2 %all-gather.3.cloned.1.call-done = f32[8192,128]{1,0:T(8,128)} async-done(((f32[128,128]{1,0:T(8,128)}), f32[8192,128]{1,0:T(8,128)}) %all-gather.3.cloned.1.call-update) | async-done | bytes 4194320 | tf_op jit(solution)/shard_map/all_gather | solution.py:42
  180.0 2.4 %reduce_sum.32 = f32[128,128]{1,0:T(8,128)S(1)} reduce(f32[64,128,128]{2,1,0:T(8,128)} %bitcast.64, f32[]{:T(128)} %constant.41.clone.1), dimensions={0}, to_apply=%region_1.2 | reduce | flops 1032192 | bytes 4259844 | tf_op jit(solution)/shard_map/reduce_sum | solution.py:43
  182.4 3.3 %collective-permute-start.1 = (f32[128,128]{1,0:T(8,128)S(1)}, f32[128,128]{1,0:T(8,128)S(1)}, u32[]{:S(2)}, u32[]{:S(2)}) collective-permute-start(f32[128,128]{1,0:T(8,128)S(1)} %reduce_sum.32), channel_id=1, source_target_pairs={{0,1},{1,0},{2,3},{3,2},{4,5},{5,4},{6,7},{7,6},{8,9},{9,8},{10,11... | collective-permute-start | bytes 196616 | tf_op jit(solution)/shard_map/ppermute | solution.py:27
  185.7 1.7 collective-permute-done.1
  187.4 0.6 select_reduce_fusion
  188.8 0.2 fusion.4
  189.0 0.2 fusion.9
  189.2 0.2 fusion.17
  189.4 0.2 fusion.26
  189.6 0.2 fusion.3
  189.8 0.2 fusion.28
  190.0 0.2 fusion.29
  190.2 0.2 fusion.2
  190.5 0.2 fusion.31
  190.7 0.2 fusion.32
  190.9 0.2 fusion.1
  191.1 0.2 fusion.34
  191.3 0.2 fusion.35
  191.5 0.2 fusion
  191.7 0.2 fusion.27
  191.9 0.2 fusion.30
  192.1 0.2 fusion.33
  192.3 0.8 convolution_multiply_fusion.5
  (2 shorter events, 0.0 us)
Async XLA Ops:
  7.2 8.2 %collective-permute-start = (bf16[128,128]{1,0:T(8,128)(2,1)}, bf16[128,128]{1,0:T(8,128)(2,1)S(1)}, u32[]{:S(2)}, u32[]{:S(2)}) collective-permute-start(bf16[128,128]{1,0:T(8,128)(2,1)} %bitcast.71), channel_id=1, source_target_pairs={{0,1},{1,0},{2,3},{3,2},{4,5},{5,4},{6,7},{7,6},{8,9},{9,8},{10,11... | collective-permute-start | bytes 98312 | tf_op jit(solution)/shard_map/ppermute | solution.py:27
  15.2 0.8 copy-start.1
  18.2 15.6 %copy-start = (f32[64,1,128]{2,1,0:T(1,128)S(1)}, f32[64,1,128]{2,1,0:T(1,128)}, u32[]{:S(2)}) copy-start(f32[64,1,128]{2,1,0:T(1,128)} %param.5) | copy-start | bytes 98308
  18.2 66.9 %all-to-all-start = ((f32[64,64,128]{2,1,0:T(8,128)}), f32[64,64,128]{2,1,0:T(8,128)S(1)}, u32[]{:S(2)}, u32[]{:S(2)}) async-start(f32[64,64,128]{2,1,0:T(8,128)} %bitcast.3), calls=%async_computation | async-start | bytes 4194304 | tf_op jit(solution)/shard_map/all_to_all | solution.py:37
  33.8 146.2 %all-gather.3.cloned.1.call-start = ((), (), s32[]{:S(2)}) async-start(), calls=%async_computation.1 | async-start | bytes 4259840 | tf_op jit(solution)/shard_map/all_gather | solution.py:42
  182.4 5.0 %collective-permute-start.1 = (f32[128,128]{1,0:T(8,128)S(1)}, f32[128,128]{1,0:T(8,128)S(1)}, u32[]{:S(2)}, u32[]{:S(2)}) collective-permute-start(f32[128,128]{1,0:T(8,128)S(1)} %reduce_sum.32), channel_id=1, source_target_pairs={{0,1},{1,0},{2,3},{3,2},{4,5},{5,4},{6,7},{7,6},{8,9},{9,8},{10,11... | collective-permute-start | bytes 196616 | tf_op jit(solution)/shard_map/ppermute | solution.py:27
Sparse Core Ops, SparseCore 0:
  86.9 93.0 all-gather.2
where the time goes:
time: 200 us
  waiting for transfers between devices  146 us (73%)
  starting transfers between devices  23.7 us (12%)
  between operations  15 us (8%)
  matrix products  5.77 us (3%)
  other arithmetic  5.33 us (3%)
  local copies, waits for them, and re-layouts  3.96 us (2%)
    all_gather x1, waiting for transfers between devices, gathered_total(): blocks = lax.all_gather(shard, axis)  93.2 us
    all_to_all x1, waiting for transfers between devices, sent_and_summed(): lax.all_to_all(in_blocks(shard, dim, count), axis, 0, 0, tiled=True)  51.2 us
    all_to_all x1, starting transfers between devices, sent_and_summed(): lax.all_to_all(in_blocks(shard, dim, count), axis, 0, 0, tiled=True)  15.6 us
    ppermute x2, starting transfers between devices, swapped(): return lax.ppermute(block, axis, route)  8.09 us
  transfers between devices with their start and end apart: 4, of which 3 were waited for; matrix products, arithmetic and copies ran while one was open for 2% of the time, Pallas kernels for 0%

commit v1 on v0

v1 whole, which is shorter than its diff:
```python
import math

import jax
import jax.numpy as jnp
from jax import lax
from jax.experimental import pallas as pl
from jax.experimental.pallas import tpu as pltpu
from jax.sharding import PartitionSpec as P

D_W = 8192
ITERS = 5
NX = 4
HD = 128
HALF = 64

retain = 0.95
first_coef = 3.4445
second_coef = -4.775
third_coef = 2.0315
epsilon = 1e-07
shrink = 0.2

MESH = pl.DeviceIdType.MESH
PRECISE = lax.Precision.HIGHEST


def chunk_order(chunks):
    return {1: (0,), 2: (1, 0), 4: (2, 1, 3, 0)}[chunks]


def step_kernel(
    ny, feat, keys, mom, upd, fresh_out,
    fv, fr, kv, lhs, mv, xs1, xr1, xk, xs2, xr2, ys, yr, gs, gr, hr, ag,
    load_sem, key_send, key_recv, f_send, f_recv, s1_send, s1_recv, s0_send, s0_recv,
    x2_send, x2_recv, y_send, y_recv, ga_send, ga_recv, gb_send, gb_recv, gc_send, gc_recv,
):
    chunks = ny // 2
    order = chunk_order(chunks)
    me = lax.axis_index("fsdp")
    z = lax.axis_index("tp")
    core = lax.rem(me, 2)
    chip = lax.div(me, 2)
    y = lax.rem(chip, ny)
    x = lax.div(chip, ny)
    par = lax.rem(z, 2)
    ky = lax.div(y, 2)
    zpair = z - par

    def device(xx, yy, cc, pp):
        return ((xx * ny + yy) * 2 + cc, zpair + pp)

    member = (x * 2 + core) * 2 + par

    def member_device(b):
        return device(lax.div(b, 4), y, lax.rem(lax.div(b, 2), 2), lax.rem(b, 2))

    barrier = pltpu.get_barrier_semaphore()

    def greet_member(d, carry):
        pl.semaphore_signal(
            barrier, inc=1, device_id=member_device(lax.rem(member + d, 16)), device_id_type=MESH
        )
        return carry

    def greet_column(d, carry):
        pl.semaphore_signal(
            barrier, inc=1, device_id=device(x, lax.rem(y + d, ny), core, par), device_id_type=MESH
        )
        return carry

    lax.fori_loop(1, ny, greet_column, 0)
    lax.fori_loop(1, 16, greet_member, 0)

    key_load = pltpu.make_async_copy(keys, kv.at[0, 0], load_sem.at[2])
    key_load.start()
    mom_load = pltpu.make_async_copy(mom, mv, load_sem.at[3])
    mom_load.start()

    def load_tiles(q, owner_core):
        def body(t, carry):
            k = lax.div(t, 8)
            r = lax.rem(t, 8)
            xx = lax.div(r, 2)
            j = lax.rem(r, 2)
            col = ((xx * ny + 2 * k + j) * 2 + owner_core) * HD
            pltpu.make_async_copy(
                feat.at[:, pl.ds(pl.multiple_of(col, HD), HD)], fv.at[q, k, r], load_sem.at[q]
            ).start()
            return carry

        lax.fori_loop(0, 8 * chunks, body, 0)

    load_tiles(1, 1 - core)
    load_tiles(0, core)
    key_load.wait()
    pltpu.make_async_copy(fv.at[1], fv.at[1], load_sem.at[1]).wait()

    pl.semaphore_wait(barrier, 15 + ny - 1)

    key_copies = []
    for n, (cc, pp, slot) in enumerate(
        (
            (1 - core, 1 - par, (1, 1)),
            (core, 1 - par, (1, 0)),
            (1 - core, par, (0, 1)),
        )
    ):
        copy = pltpu.make_async_remote_copy(
            src_ref=kv.at[0, 0],
            dst_ref=kv.at[slot[0], slot[1]],
            send_sem=key_send.at[n],
            recv_sem=key_recv.at[n],
            device_id=device(x, y, cc, pp),
            device_id_type=MESH,
        )
        copy.start()
        key_copies.append(copy)
    f_copies = []
    for i in range(chunks):
        k = lax.rem(ky + order[i], chunks)
        copy = pltpu.make_async_remote_copy(
            src_ref=fv.at[1, k],
            dst_ref=fr.at[k],
            send_sem=f_send.at[i],
            recv_sem=f_recv.at[i],
            device_id=device(x, y, 1 - core, par),
            device_id_type=MESH,
        )
        copy.start()
        f_copies.append(copy)

    pltpu.make_async_copy(fv.at[0], fv.at[0], load_sem.at[0]).wait()
    for copy in key_copies:
        copy.wait_recv()
    for r in range(2):
        for f in range(2):
            lhs[r * HD : (r + 1) * HD, f * HD : (f + 1) * HD] = kv[r, f].T

    lane = lax.broadcasted_iota(jnp.int32, (HD, HD), 1)
    kept = jnp.logical_and(lane >= HALF * par, lane < HALF * par + HALF)

    def partial_for(k, dest):
        top = jnp.concatenate([fv[0, k, 2 * dest], fv[0, k, 2 * dest + 1]], axis=1)
        bottom = jnp.concatenate([fr[k, 2 * dest], fr[k, 2 * dest + 1]], axis=1)
        rhs = jnp.concatenate([top, bottom], axis=0)
        both = jnp.dot(lhs[...], rhs, preferred_element_type=jnp.float32)
        both = both[:HD] + both[HD:]
        low, high = both[:, :HD], both[:, HD:]
        still = jnp.where(par == 0, low, high)
        moved = jnp.where(par == 0, high, low)
        return jnp.where(kept, still, pltpu.roll(moved, HALF, axis=1))

    near = (x + 1 - 2 * lax.rem(x, 2), 3 - x)
    across = lax.rem(x + 2, NX)

    def first(i):
        return near[i % 2]

    def second(i):
        return near[1 - i % 2]

    def chunk(i):
        return lax.rem(ky + order[i], chunks)

    def send(src, dst, send_sem, recv_sem, target):
        copy = pltpu.make_async_remote_copy(
            src_ref=src,
            dst_ref=dst,
            send_sem=send_sem,
            recv_sem=recv_sem,
            device_id=target,
            device_id_type=MESH,
        )
        copy.start()
        return copy

    s1, s0, x2, ysends = {}, {}, {}, []

    def send_far(i):
        s1[i] = send(
            xs1.at[i, 1], xr1.at[i, 1], s1_send.at[i], s1_recv.at[i], device(first(i), y, core, par)
        )

    def send_near(i):
        s0[i] = send(
            xs1.at[i, 0], xr1.at[i, 0], s0_send.at[i], s0_recv.at[i], device(first(i), y, core, par)
        )

    def forward(i):
        s1[i].wait_recv()
        xs2[i] = xk[i, 0] + xr1[i, 1]
        x2[i] = send(xs2.at[i], xr2.at[i], x2_send.at[i], x2_recv.at[i], device(second(i), y, core, par))

    def finish(i):
        s0[i].wait_recv()
        x2[i].wait_recv()
        ys[i] = (xk[i, 1] + xr1[i, 0] + xr2[i]).T
        k = chunk(i)
        if order[i] == 0:
            j = 1 - lax.rem(y, 2)
            targets = [(2 * ky + j, j)]
        else:
            targets = [(2 * k, 0), (2 * k + 1, 1)]
        for yy, j in targets:
            ysends.append(
                send(
                    ys.at[i, pl.ds(pl.multiple_of(j * HALF, HALF), HALF)],
                    yr.at[y],
                    y_send.at[len(ysends)],
                    y_recv.at[y],
                    device(x, yy, core, par),
                )
            )

    lead = list(range(min(2, chunks)))
    rest = list(range(len(lead), chunks))
    for i in lead:
        f_copies[i].wait_recv()
        xs1[i, 1] = partial_for(chunk(i), across)
        send_far(i)
    for i in lead:
        xs1[i, 0] = partial_for(chunk(i), first(i))
        send_near(i)
    for i in rest:
        f_copies[i].wait_recv()
        xs1[i, 1] = partial_for(chunk(i), across)
        send_far(i)
    for i in lead:
        xk[i, 0] = partial_for(chunk(i), second(i))
    for i in rest:
        xs1[i, 0] = partial_for(chunk(i), first(i))
    for i in lead:
        forward(i)
    for i in rest:
        send_near(i)
    for i in rest:
        xk[i, 0] = partial_for(chunk(i), second(i))
    for i in lead + rest:
        xk[i, 1] = partial_for(chunk(i), x)
    for i in rest:
        forward(i)
    for i in lead + rest:
        finish(i)

    mom_load.wait()
    last = len(order) - 1
    grads = ys[last, pl.ds(pl.multiple_of(lax.rem(y, 2) * HALF, HALF), HALF), :]
    for d in range(1, ny):
        yy = lax.rem(y + d, ny)
        pltpu.make_async_remote_copy(
            src_ref=yr.at[yy],
            dst_ref=yr.at[yy],
            send_sem=y_send.at[0],
            recv_sem=y_recv.at[yy],
            device_id=device(x, yy, core, par),
            device_id_type=MESH,
        ).wait_recv()
        grads = grads + yr[yy]

    fresh = retain * mv[...] + grads
    fresh_out[...] = fresh
    blend = grads + retain * fresh
    contract = (((0,), (0,)), ((), ()))
    gs[...] = lax.dot_general(
        blend, blend, contract, precision=PRECISE, preferred_element_type=jnp.float32
    )

    def piece(b):
        return pl.ds(pl.multiple_of(b * 8, 8), 8)

    def scatter(d, carry):
        b = lax.rem(member + d, 16)
        pltpu.make_async_remote_copy(
            src_ref=gs.at[piece(b)],
            dst_ref=gr.at[member],
            send_sem=ga_send.at[b],
            recv_sem=ga_recv.at[member],
            device_id=member_device(b),
            device_id_type=MESH,
        ).start()
        return carry

    lax.fori_loop(1, 16, scatter, 0)
    gr[member] = gs[piece(member), :]

    def scatter_wait(d, carry):
        b = lax.rem(member + d, 16)
        copy = pltpu.make_async_remote_copy(
            src_ref=gs.at[piece(b)],
            dst_ref=gr.at[b],
            send_sem=ga_send.at[b],
            recv_sem=ga_recv.at[b],
            device_id=member_device(b),
            device_id_type=MESH,
        )
        copy.wait_recv()
        return carry

    lax.fori_loop(1, 16, scatter_wait, 0)
    hr[y] = jnp.sum(gr[...], axis=0)

    def column(d, carry):
        yy = lax.rem(y + d, ny)
        pltpu.make_async_remote_copy(
            src_ref=hr.at[y],
            dst_ref=hr.at[y],
            send_sem=gb_send.at[yy],
            recv_sem=gb_recv.at[y],
            device_id=device(x, yy, core, par),
            device_id_type=MESH,
        ).start()
        return carry

    lax.fori_loop(1, ny, column, 0)

    def column_wait(d, carry):
        yy = lax.rem(y + d, ny)
        pltpu.make_async_remote_copy(
            src_ref=hr.at[y],
            dst_ref=hr.at[yy],
            send_sem=gb_send.at[yy],
            recv_sem=gb_recv.at[yy],
            device_id=device(x, yy, core, par),
            device_id_type=MESH,
        ).wait_recv()
        return carry

    lax.fori_loop(1, ny, column_wait, 0)
    ag[member] = jnp.sum(hr[...], axis=0)

    def gather(d, carry):
        b = lax.rem(member + d, 16)
        pltpu.make_async_remote_copy(
            src_ref=ag.at[member],
            dst_ref=ag.at[member],
            send_sem=gc_send.at[b],
            recv_sem=gc_recv.at[member],
            device_id=member_device(b),
            device_id_type=MESH,
        ).start()
        return carry

    lax.fori_loop(1, 16, gather, 0)

    def gather_wait(d, carry):
        b = lax.rem(member + d, 16)
        pltpu.make_async_remote_copy(
            src_ref=ag.at[member],
            dst_ref=ag.at[b],
            send_sem=gc_send.at[b],
            recv_sem=gc_recv.at[b],
            device_id=member_device(b),
            device_id_type=MESH,
        ).wait_recv()
        return carry

    lax.fori_loop(1, 16, gather_wait, 0)

    gram = ag[...].reshape(HD, HD)
    row = lax.broadcasted_iota(jnp.int32, (HD, HD), 0)
    identity = jnp.where(row == lane, 1.0, 0.0).astype(jnp.float32)
    total = jnp.sum(gram * identity, axis=(0, 1), keepdims=True)
    inverse = 1.0 / (jnp.sqrt(total) + epsilon)

    def dot(a, b):
        return jnp.dot(a, b, precision=PRECISE, preferred_element_type=jnp.float32)

    state = blend * inverse
    gram = gram * (inverse * inverse)
    for step in range(ITERS):
        square = dot(gram, gram)
        poly = first_coef * identity + second_coef * gram + third_coef * square
        state = dot(state, poly)
        if step < ITERS - 1:
            gram = dot(dot(gram, poly), poly)
    upd[...] = shrink * math.sqrt(D_W) * state

    for copy in key_copies + f_copies + ysends:
        copy.wait_send()
    for group in (s1, s0, x2):
        for copy in group.values():
            copy.wait_send()

    def drain_members(d, carry):
        b = lax.rem(member + d, 16)
        for src, sem in ((gs.at[piece(b)], ga_send), (ag.at[member], gc_send)):
            pltpu.make_async_remote_copy(
                src_ref=src,
                dst_ref=gr.at[member],
                send_sem=sem.at[b],
                recv_sem=ga_recv.at[member],
                device_id=member_device(b),
                device_id_type=MESH,
            ).wait_send()
        return carry

    lax.fori_loop(1, 16, drain_members, 0)

    def drain_column(d, carry):
        yy = lax.rem(y + d, ny)
        pltpu.make_async_remote_copy(
            src_ref=hr.at[y],
            dst_ref=hr.at[y],
            send_sem=gb_send.at[yy],
            recv_sem=gb_recv.at[y],
            device_id=device(x, yy, core, par),
            device_id_type=MESH,
        ).wait_send()
        return carry

    lax.fori_loop(1, ny, drain_column, 0)


def on_device(features, key_partials, momentum):
    ny = lax.axis_size("fsdp") // (2 * NX)
    chunks = ny // 2
    f32, bf16 = jnp.float32, jnp.bfloat16
    dma = pltpu.SemaphoreType.DMA
    block = jax.ShapeDtypeStruct((HALF, HD), f32)
    anywhere = pl.BlockSpec(memory_space=pl.ANY)
    vmem = pl.BlockSpec(memory_space=pltpu.VMEM)

    def body(*refs):
        step_kernel(ny, *refs)

    update, fresh = pl.pallas_call(
        body,
        name="muon_step",
        out_shape=(block, block),
        in_specs=[anywhere] * 3,
        out_specs=(vmem, vmem),
        scratch_shapes=[
            pltpu.VMEM((2, chunks, 8, HD, HD), bf16),
            pltpu.VMEM((chunks, 8, HD, HD), bf16),
            pltpu.VMEM((2, 2, HD, HD), bf16),
            pltpu.VMEM((2 * HD, 2 * HD), bf16),
            pltpu.VMEM((HALF, HD), f32),
            pltpu.VMEM((chunks, 2, HD, HD), f32),
            pltpu.VMEM((chunks, 2, HD, HD), f32),
            pltpu.VMEM((chunks, 2, HD, HD), f32),
            pltpu.VMEM((chunks, HD, HD), f32),
            pltpu.VMEM((chunks, HD, HD), f32),
            pltpu.VMEM((chunks, HD, HD), f32),
            pltpu.VMEM((ny, HALF, HD), f32),
            pltpu.VMEM((HD, HD), f32),
            pltpu.VMEM((16, 8, HD), f32),
            pltpu.VMEM((ny, 8, HD), f32),
            pltpu.VMEM((16, 8, HD), f32),
            dma((4,)),
            dma((3,)), dma((3,)),
            dma((chunks,)), dma((chunks,)),
            dma((chunks,)), dma((chunks,)),
            dma((chunks,)), dma((chunks,)),
            dma((chunks,)), dma((chunks,)),
            dma((ny,)), dma((ny,)),
            dma((16,)), dma((16,)),
            dma((ny,)), dma((ny,)),
            dma((16,)), dma((16,)),
        ],
        compiler_params=pltpu.CompilerParams(collective_id=0, has_side_effects=True),
    )(features, key_partials[:, 0, :], momentum[:, 0, :])
    return (update[:, None, :], fresh[:, None, :])


def solution(mesh):
    placed = (P("fsdp", None), P("fsdp", "tp", None), P("fsdp", "tp", None))
    return jax.shard_map(
        on_device,
        mesh=mesh,
        in_specs=placed,
        out_specs=(P("fsdp", "tp", None), P("fsdp", "tp", None)),
        check_vma=False,
    )
```

time: 200 us -> 58.5 us (0.29)
  waiting for transfers between devices: 146 us -> 0 us
  Pallas kernels: 0 us -> 54.7 us
  starting transfers between devices: 23.7 us -> 0 us
  between operations: 15 us -> 0.64 us
  matrix products: 5.77 us -> 0 us
  other arithmetic: 5.33 us -> 0 us
    all_gather x1 -> x0, waiting for transfers between devices: 93.2 us -> none  [gathered_total(): blocks = lax.all_gather(shard, axis)]
    pallas_call x0 -> x1, Pallas kernels: none -> 54.7 us  [on_device(): pl.pallas_call(body, name='muon_step', out_shape=(block, block), in_specs...]
    all_to_all x1 -> x0, waiting for transfers between devices: 51.2 us -> none  [sent_and_summed(): lax.all_to_all(in_blocks(shard, dim, count), axis, 0, 0, tiled=True)]
    all_to_all x1 -> x0, starting transfers between devices: 15.6 us -> none  [sent_and_summed(): lax.all_to_all(in_blocks(shard, dim, count), axis, 0, 0, tiled=True)]
    ppermute x2 -> x0, starting transfers between devices: 8.09 us -> none  [swapped(): return lax.ppermute(block, axis, route)]
    dot_general x20 -> x0, matrix products: 5.77 us -> none  [the longest x5 1.54 us: on_device(): state = jnp.dot(state, poly, precision=precise)]
    reduce_sum x3 -> x0, other arithmetic: 3.16 us -> none  [the longest x1 2.41 us: gathered_total(): return blocks.sum(axis=0)]
    add x2 -> x0, other arithmetic: 2.17 us -> none  [the longest x1 1.54 us: on_device(): product[:, :head_size] + product[:, head_size:]]
  transfers between devices with their start and end apart: 4 -> 0, of which waited for: 3 -> 0; matrix products, arithmetic and copies ran while one was open for 2% -> 0% of each run, Pallas kernels for 0% -> 0%
where the time goes in v1:
time: 58.5 us; the launch traced here: 58.1 us
  Pallas kernels  54.7 us (94%)
  local copies, waits for them, and re-layouts  2.75 us (5%)
  between operations  0.64 us (1%)
    pallas_call x1, Pallas kernels, on_device(): pl.pallas_call(body, name='muon_step', out_shape=(block, block), in_specs...  54.7 us
    unnamed x2, local copies, waits for them, and re-layouts  2.75 us

profile of v1, /device:TPU:1, one launch (start us, length us, event | category | flops | bytes accessed | tf_op | source)
XLA Modules:
  0.0 58.1 jit_solution(14426646397062735647)
XLA Ops:
  0.6 54.7 %muon_step.1 = (f32[64,128]{1,0:T(8,128)}, f32[64,128]{1,0:T(8,128)}) custom-call(bf16[128,8192]{1,0:T(8,128)(2,1)} %refs_0_.1, bf16[128,128]{1,0:T(8,128)(2,1)} %bitcast.8, f32[64,128]{1,0:T(8,128)} %bitcast.9), custom_call_target="tpu_custom_call" | custom-call | tf_op jit(solution)/shard_map/muon_step/pallas_call | solution.py:426
  55.3 1.4 %copy.9 = f32[64,1,128]{2,1,0:T(1,128)} copy(f32[64,1,128]{2,1,0:T(1,128)} %bitcast.11) | data formatting | bytes 65536
  56.7 1.4 %copy.10 = f32[64,1,128]{2,1,0:T(1,128)} copy(f32[64,1,128]{2,1,0:T(1,128)} %bitcast.10) | data formatting | bytes 65536

commit v2 on v0

v2 whole, which is shorter than its diff:
```python
import math

import jax
import jax.numpy as jnp
from jax import lax
from jax.experimental import pallas as pl
from jax.experimental.pallas import tpu as pltpu
from jax.sharding import PartitionSpec as P

D_W = 8192
ITERS = 5
NX = 4
HD = 128
HALF = 64

retain = 0.95
first_coef = 3.4445
second_coef = -4.775
third_coef = 2.0315
epsilon = 1e-07
shrink = 0.2

MESH = pl.DeviceIdType.MESH
PRECISE = lax.Precision.HIGHEST


def chunk_order(chunks):
    return {1: (0,), 2: (1, 0), 4: (2, 1, 3, 0)}[chunks]


def step_kernel(
    ny, feat, keys, mom, state_out, grads_out,
    fv, fr, kv, lhs, mv, sf, pn, px, rx, fw, ys, yr, gs, gr, hr, ag,
    load_sem, key_sem, f_send, f_recv, x_send, x_recv, y_send, y_recv, g_send, g_recv,
):
    chunks = ny // 2
    order = chunk_order(chunks)
    me = lax.axis_index("fsdp")
    z = lax.axis_index("tp")
    core = lax.rem(me, 2)
    chip = lax.div(me, 2)
    y = lax.rem(chip, ny)
    x = lax.div(chip, ny)
    par = lax.rem(z, 2)
    ky = lax.div(y, 2)
    zpair = z - par

    xs = [x] + [lax.rem(x + d, NX) for d in range(1, NX)]
    yy = [y] + [lax.rem(y + d, ny) for d in range(1, ny)]
    cs = (core, 1 - core)
    ps = (par, 1 - par)

    def device(xx, yv, cc, pp):
        return ((xx * ny + yv) * 2 + cc, zpair + pp)

    def number(xx, cc, pp):
        return (xx * 2 + cc) * 2 + pp

    member = number(x, core, par)
    others = [
        (xs[dx], cs[dc], ps[dp])
        for dx in (2, 1, 3, 0)
        for dp in (1, 0)
        for dc in (1, 0)
        if (dx, dp, dc) != (0, 0, 0)
    ]
    far_first = sorted(range(1, ny), key=lambda d: -min(d, ny - d))

    def start(src, dst, send_sem, recv_sem, target):
        pltpu.make_async_remote_copy(
            src_ref=src,
            dst_ref=dst,
            send_sem=send_sem,
            recv_sem=recv_sem,
            device_id=target,
            device_id_type=MESH,
        ).start()

    def await_bytes(ref, sem):
        pltpu.make_async_copy(ref, ref, sem).wait()

    key_load = pltpu.make_async_copy(keys, kv.at[0], load_sem.at[chunks])
    key_load.start()
    barrier = pltpu.get_barrier_semaphore()
    for d in far_first:
        pl.semaphore_signal(
            barrier, inc=1, device_id=device(x, yy[d], core, par), device_id_type=MESH
        )
    for xx, cc, pp in others:
        pl.semaphore_signal(barrier, inc=1, device_id=device(xx, y, cc, pp), device_id_type=MESH)

    def chunk(i):
        return lax.rem(ky + order[i], chunks)

    ks = [chunk(i) for i in range(chunks)]

    wide = 4 * HD
    for i in range(chunks):
        for xx in range(NX):
            col = pl.multiple_of((xx * ny + 2 * ks[i]) * 2 * HD, wide)
            pltpu.make_async_copy(
                feat.at[:, pl.ds(col, wide)], fv.at[ks[i], xx], load_sem.at[i]
            ).start()
    mom_load = pltpu.make_async_copy(mom, mv, load_sem.at[chunks + 1])
    mom_load.start()

    key_load.wait()
    pl.semaphore_wait(barrier, 15 + ny - 1)

    for cc, pp, slot in ((cs[1], ps[1], 3), (core, ps[1], 2), (cs[1], par, 1)):
        start(kv.at[0], kv.at[slot], key_sem.at[0], key_sem.at[1], device(x, y, cc, pp))
    for i in range(chunks):
        await_bytes(fv.at[ks[i]], load_sem.at[i])
        for xx in (2, 1, 3, 0):
            for j in range(2):
                col = pl.multiple_of((2 * j + 1 - core) * HD, HD)
                start(
                    fv.at[ks[i], xs[xx], :, pl.ds(col, HD)],
                    fr.at[ks[i], xs[xx], :, pl.ds(j * HD, HD)],
                    f_send.at[0],
                    f_recv.at[i],
                    device(x, y, 1 - core, par),
                )

    await_bytes(kv.at[pl.ds(1, 3)], key_sem.at[1])
    for r in range(2):
        for f in range(2):
            lhs[r * HD : (r + 1) * HD, f * HD : (f + 1) * HD] = kv[2 * r + f].T

    lane = lax.broadcasted_iota(jnp.int32, (HD, HD), 1)
    kept = jnp.logical_and(lane >= HALF * par, lane < HALF * par + HALF)
    first_tile = pl.ds(pl.multiple_of(core * HD, HD), HD)
    second_tile = pl.ds(pl.multiple_of((2 + core) * HD, HD), HD)

    def partial_for(k, dest):
        top = jnp.concatenate([fv[k, dest, :, first_tile], fv[k, dest, :, second_tile]], axis=1)
        rhs = jnp.concatenate([top, fr[k, dest]], axis=0)
        both = jnp.dot(lhs[...], rhs, preferred_element_type=jnp.float32)
        both = both[:HD] + both[HD:]
        low, high = both[:, :HD], both[:, HD:]
        still = jnp.where(par == 0, low, high)
        moved = jnp.where(par == 0, high, low)
        return jnp.where(kept, still, pltpu.roll(moved, HALF, axis=1))

    near = (x + 1 - 2 * lax.rem(x, 2), 3 - x)
    halves = (pl.ds(0, HALF), pl.ds(HALF, HALF))

    def step_one(i):
        await_bytes(fr.at[ks[i]], f_recv.at[i])
        sf[i] = partial_for(ks[i], xs[2])
        for h in range(2):
            start(
                sf.at[i, halves[h]], rx.at[0, i, h], x_send.at[0], x_recv.at[0, i, h],
                device(near[h], y, core, par),
            )
        for a in range(2):
            pn[i, a] = partial_for(ks[i], near[a])
        for h in range(2):
            start(
                pn.at[i, h, halves[h]], rx.at[1, i, h], x_send.at[0], x_recv.at[1, i, h],
                device(near[h], y, core, par),
            )

    def step_two(i):
        for h in range(2):
            await_bytes(rx.at[0, i, h], x_recv.at[0, i, h])
            fw[i, h] = pn[i, 1 - h, halves[h], :] + rx[0, i, h]
            start(
                fw.at[i, h], rx.at[2, i, h], x_send.at[0], x_recv.at[2, i, h],
                device(near[1 - h], y, core, par),
            )

    def own(i):
        px[i] = partial_for(ks[i], x)

    def finish(i):
        for stage in (1, 2):
            for h in range(2):
                await_bytes(rx.at[stage, i, h], x_recv.at[stage, i, h])
        total = px[i] + (rx[1, i] + rx[2, i]).reshape(HD, HD)
        ys[i] = total.T
        if order[i] == 0:
            j = 1 - lax.rem(y, 2)
            targets = [(2 * ky + j, j)]
        else:
            targets = [(2 * ks[i], 0), (2 * ks[i] + 1, 1)]
        for yv, j in targets:
            rows = pl.ds(pl.multiple_of(j * HALF, HALF), HALF)
            start(ys.at[i, rows], yr.at[y], y_send.at[0], y_recv.at[y], device(x, yv, core, par))

    if chunks == 4:
        step_one(0)
        step_one(1)
        step_two(0)
        step_one(2)
        step_two(1)
        step_one(3)
        for i in range(chunks):
            own(i)
        finish(0)
        step_two(2)
        finish(1)
        step_two(3)
        finish(2)
        finish(3)
    else:
        for i in range(chunks):
            step_one(i)
        for i in range(chunks):
            step_two(i)
            own(i)
        for i in range(chunks):
            finish(i)

    mom_load.wait()
    grads = ys[chunks - 1, pl.ds(pl.multiple_of(lax.rem(y, 2) * HALF, HALF), HALF), :]
    for d in far_first:
        await_bytes(yr.at[yy[d]], y_recv.at[yy[d]])
        grads = grads + yr[yy[d]]

    grads_out[...] = grads
    blend = grads + retain * (retain * mv[...] + grads)
    contract = (((0,), (0,)), ((), ()))
    gs[...] = lax.dot_general(
        blend, blend, contract, precision=PRECISE, preferred_element_type=jnp.float32
    )

    def piece(b):
        return pl.ds(pl.multiple_of(b * 8, 8), 8)

    for xx, cc, pp in others:
        start(
            gs.at[piece(number(xx, cc, pp))], gr.at[member], g_send.at[0], g_recv.at[0],
            device(xx, y, cc, pp),
        )
    gr[member] = gs[piece(member), :]
    await_bytes(gr.at[pl.ds(0, 15)], g_recv.at[0])
    hr[y] = jnp.sum(gr[...], axis=0)
    for d in far_first:
        start(hr.at[y], hr.at[y], g_send.at[1], g_recv.at[1], device(x, yy[d], core, par))
    await_bytes(hr.at[pl.ds(0, ny - 1)], g_recv.at[1])
    ag[member] = jnp.sum(hr[...], axis=0)
    for xx, cc, pp in others:
        start(
            ag.at[member], ag.at[member], g_send.at[2], g_recv.at[2], device(xx, y, cc, pp)
        )
    await_bytes(ag.at[pl.ds(0, 15)], g_recv.at[2])

    gram = ag[...].reshape(HD, HD)
    row = lax.broadcasted_iota(jnp.int32, (HD, HD), 0)
    identity = jnp.where(row == lane, 1.0, 0.0).astype(jnp.float32)
    total = jnp.sum(gram * identity, axis=(0, 1), keepdims=True)
    inverse = 1.0 / (jnp.sqrt(total) + epsilon)

    def dot(a, b):
        return jnp.dot(a, b, precision=PRECISE, preferred_element_type=jnp.float32)

    state = blend * inverse
    gram = gram * (inverse * inverse)
    for step in range(ITERS):
        square = dot(gram, gram)
        poly = first_coef * identity + second_coef * gram + third_coef * square
        state = dot(state, poly)
        if step < ITERS - 1:
            gram = dot(dot(gram, poly), poly)
    state_out[...] = state

    await_bytes(kv.at[pl.ds(1, 3)], key_sem.at[0])
    await_bytes(fr, f_send.at[0])
    await_bytes(rx, x_send.at[0])
    await_bytes(yr.at[pl.ds(0, ny - 1)], y_send.at[0])
    await_bytes(gr.at[pl.ds(0, 15)], g_send.at[0])
    await_bytes(hr.at[pl.ds(0, ny - 1)], g_send.at[1])
    await_bytes(ag.at[pl.ds(0, 15)], g_send.at[2])


def on_device(features, key_partials, momentum):
    ny = lax.axis_size("fsdp") // (2 * NX)
    chunks = ny // 2
    f32, bf16 = jnp.float32, jnp.bfloat16
    dma = pltpu.SemaphoreType.DMA
    block = jax.ShapeDtypeStruct((HALF, HD), f32)
    hbm = pl.BlockSpec(memory_space=pltpu.HBM)
    vmem = pl.BlockSpec(memory_space=pltpu.VMEM)
    moment = momentum[:, 0, :]

    def body(*refs):
        step_kernel(ny, *refs)

    state, grads = pl.pallas_call(
        body,
        name="muon_step",
        out_shape=(block, block),
        in_specs=[hbm] * 3,
        out_specs=(vmem, vmem),
        scratch_shapes=[
            pltpu.VMEM((chunks, NX, HD, 4 * HD), bf16),
            pltpu.VMEM((chunks, NX, HD, 2 * HD), bf16),
            pltpu.VMEM((4, HD, HD), bf16),
            pltpu.VMEM((2 * HD, 2 * HD), bf16),
            pltpu.VMEM((HALF, HD), f32),
            pltpu.VMEM((chunks, HD, HD), f32),
            pltpu.VMEM((chunks, 2, HD, HD), f32),
            pltpu.VMEM((chunks, HD, HD), f32),
            pltpu.VMEM((3, chunks, 2, HALF, HD), f32),
            pltpu.VMEM((chunks, 2, HALF, HD), f32),
            pltpu.VMEM((chunks, HD, HD), f32),
            pltpu.VMEM((ny, HALF, HD), f32),
            pltpu.VMEM((HD, HD), f32),
            pltpu.VMEM((16, 8, HD), f32),
            pltpu.VMEM((ny, 8, HD), f32),
            pltpu.VMEM((16, 8, HD), f32),
            dma((chunks + 2,)),
            dma((2,)),
            dma((1,)), dma((chunks,)),
            dma((1,)), dma((3, chunks, 2)),
            dma((1,)), dma((ny,)),
            dma((3,)), dma((3,)),
        ],
        compiler_params=pltpu.CompilerParams(
            collective_id=0, has_side_effects=True, vmem_limit_bytes=16 * 1024 * 1024
        ),
    )(*(pltpu.with_memory_space_constraint(v, pltpu.HBM) for v in (features, key_partials[:, 0, :], moment)))
    update = shrink * math.sqrt(D_W) * state
    return (update[:, None, :], (retain * moment + grads)[:, None, :])


def solution(mesh):
    placed = (P("fsdp", None), P("fsdp", "tp", None), P("fsdp", "tp", None))
    return jax.shard_map(
        on_device,
        mesh=mesh,
        in_specs=placed,
        out_specs=(P("fsdp", "tp", None), P("fsdp", "tp", None)),
        check_vma=False,
    )
```

time: 200 us -> 53.6 us (0.27)
  waiting for transfers between devices: 146 us -> 0 us
  Pallas kernels: 0 us -> 52.1 us
  starting transfers between devices: 23.7 us -> 0 us
  between operations: 15 us -> 0.65 us
  matrix products: 5.77 us -> 0 us
  other arithmetic: 5.33 us -> 0.63 us
  local copies, waits for them, and re-layouts: 3.96 us -> 0.01 us
    all_gather x1 -> x0, waiting for transfers between devices: 93.2 us -> none  [gathered_total(): blocks = lax.all_gather(shard, axis)]
    pallas_call x0 -> x1, Pallas kernels: none -> 52.1 us  [on_device(): pl.pallas_call(body, name='muon_step', out_shape=(block, block), in_specs...]
    all_to_all x1 -> x0, waiting for transfers between devices: 51.2 us -> none  [sent_and_summed(): lax.all_to_all(in_blocks(shard, dim, count), axis, 0, 0, tiled=True)]
    all_to_all x1 -> x0, starting transfers between devices: 15.6 us -> none  [sent_and_summed(): lax.all_to_all(in_blocks(shard, dim, count), axis, 0, 0, tiled=True)]
    ppermute x2 -> x0, starting transfers between devices: 8.09 us -> none  [swapped(): return lax.ppermute(block, axis, route)]
    dot_general x20 -> x0, matrix products: 5.77 us -> none  [the longest x5 1.54 us: on_device(): state = jnp.dot(state, poly, precision=precise)]
    unnamed x5 -> x2, local copies, waits for them, and re-layouts: 3.86 us -> 0.01 us
    reduce_sum x3 -> x0, other arithmetic: 3.16 us -> none  [the longest x1 2.41 us: gathered_total(): return blocks.sum(axis=0)]
  transfers between devices with their start and end apart: 4 -> 0, of which waited for: 3 -> 0; matrix products, arithmetic and copies ran while one was open for 2% -> 0% of each run, Pallas kernels for 0% -> 0%
where the time goes in v2:
time: 53.6 us; the launch traced here: 53.4 us
  Pallas kernels  52.1 us (97%)
  between operations  0.65 us (1%)
  other arithmetic  0.63 us (1%)
    pallas_call x1, Pallas kernels, on_device(): pl.pallas_call(body, name='muon_step', out_shape=(block, block), in_specs...  52.1 us

profile of v2, /device:TPU:1, one launch (start us, length us, event | category | flops | bytes accessed | tf_op | source)
XLA Modules:
  0.0 53.4 jit_solution(2126142551969832663)
XLA Ops:
  0.6 0.0 copy-start
  0.6 52.1 %muon_step.1 = (f32[64,128]{1,0:T(8,128)S(1)}, f32[64,128]{1,0:T(8,128)S(1)}) custom-call(bf16[128,8192]{1,0:T(8,128)(2,1)} %refs_0_.1, bf16[128,128]{1,0:T(8,128)(2,1)} %bitcast.10, f32[64,128]{1,0:T(8,128)} %bitcast.8), custom_call_target="tpu_custom_call" | custom-call | tf_op jit(solution)/shard_map/muon_step/pallas_call | solution.py:290
  52.7 0.0 copy-done
  52.7 0.6 %multiply_add_fusion = (f32[64,128]{1,0:T(8,128)}, f32[64,128]{1,0:T(8,128)}) fusion(f32[64,128]{1,0:T(8,128)S(1)} %get-tuple-element.5, f32[64,128]{1,0:T(8,128)S(1)} %bitcast.9, f32[64,128]{1,0:T(8,128)S(1)} %get-tuple-element.4), kind=kLoop, calls=%fused_computation | loop fusion | flops 24576 | bytes 163840 | tf_op jit(solution)/shard_map/add | solution.py:325
Async XLA Ops:
  0.6 52.1 %copy-start = (f32[64,1,128]{2,1,0:T(1,128)S(1)}, f32[64,1,128]{2,1,0:T(1,128)}, u32[]{:S(2)}) copy-start(f32[64,1,128]{2,1,0:T(1,128)} %param.5) | copy-start | bytes 98308

commit v3 on v2

--- a/solution.py
+++ b/solution.py
@@ -30,8 +30,9 @@
 
 def step_kernel(
     ny, feat, keys, mom, state_out, grads_out,
-    fv, fr, kv, lhs, mv, sf, pn, px, rx, fw, ys, yr, gs, gr, hr, ag,
-    load_sem, key_sem, f_send, f_recv, x_send, x_recv, y_send, y_recv, g_send, g_recv,
+    fv, fr, kv, lhs, mv, sf, pn, px, rx, fw, ys, yr, sy, ry, sk, qs, xd, gs, gr, hr, ag,
+    load_sem, key_sem, f_send, f_recv, x_send, x_recv, y_send, y_recv, p_send, p_recv, d_send, d_recv,
+    g_send, g_recv,
 ):
     chunks = ny // 2
     order = chunk_order(chunks)
@@ -129,12 +130,14 @@
 
     lane = lax.broadcasted_iota(jnp.int32, (HD, HD), 1)
     kept = jnp.logical_and(lane >= HALF * par, lane < HALF * par + HALF)
-    first_tile = pl.ds(pl.multiple_of(core * HD, HD), HD)
-    second_tile = pl.ds(pl.multiple_of((2 + core) * HD, HD), HD)
-
-    def partial_for(k, dest):
-        top = jnp.concatenate([fv[k, dest, :, first_tile], fv[k, dest, :, second_tile]], axis=1)
-        rhs = jnp.concatenate([top, fr[k, dest]], axis=0)
+
+    def tiles(k, dest, j):
+        own_lanes = pl.ds(pl.multiple_of((2 * j + core) * HD, HD), HD)
+        other_lanes = pl.ds(pl.multiple_of(j * HD, HD), HD)
+        return jnp.concatenate([fv[k, dest, :, own_lanes], fr[k, dest, :, other_lanes]], axis=0)
+
+    def partial_pair(k, dest_low, j_low, dest_high, j_high):
+        rhs = jnp.concatenate([tiles(k, dest_low, j_low), tiles(k, dest_high, j_high)], axis=1)
         both = jnp.dot(lhs[...], rhs, preferred_element_type=jnp.float32)
         both = both[:HD] + both[HD:]
         low, high = both[:, :HD], both[:, HD:]
@@ -142,10 +145,13 @@
         moved = jnp.where(par == 0, high, low)
         return jnp.where(kept, still, pltpu.roll(moved, HALF, axis=1))
 
+    def partial_for(k, dest):
+        return partial_pair(k, dest, 0, dest, 1)
+
     near = (x + 1 - 2 * lax.rem(x, 2), 3 - x)
     halves = (pl.ds(0, HALF), pl.ds(HALF, HALF))
 
-    def step_one(i):
+    def send_far(i):
         await_bytes(fr.at[ks[i]], f_recv.at[i])
         sf[i] = partial_for(ks[i], xs[2])
         for h in range(2):
@@ -153,6 +159,8 @@
                 sf.at[i, halves[h]], rx.at[0, i, h], x_send.at[0], x_recv.at[0, i, h],
                 device(near[h], y, core, par),
             )
+
+    def send_near(i):
         for a in range(2):
             pn[i, a] = partial_for(ks[i], near[a])
         for h in range(2):
@@ -179,44 +187,76 @@
                 await_bytes(rx.at[stage, i, h], x_recv.at[stage, i, h])
         total = px[i] + (rx[1, i] + rx[2, i]).reshape(HD, HD)
         ys[i] = total.T
-        if order[i] == 0:
-            j = 1 - lax.rem(y, 2)
-            targets = [(2 * ky + j, j)]
-        else:
-            targets = [(2 * ks[i], 0), (2 * ks[i] + 1, 1)]
-        for yv, j in targets:
-            rows = pl.ds(pl.multiple_of(j * HALF, HALF), HALF)
-            start(ys.at[i, rows], yr.at[y], y_send.at[0], y_recv.at[y], device(x, yv, core, par))
-
+        for j in range(2):
+            yv = 2 * ks[i] + j
+            start(ys.at[i, halves[j]], yr.at[y], y_send.at[0], y_recv.at[y], device(x, yv, core, par))
+
+    mine = lax.rem(y, 2)
+    beside = 2 * ky + 1 - mine
+    last = chunks - 1
+
+    def send_pair():
+        await_bytes(fr.at[ks[last]], f_recv.at[last])
+        for m in range(2):
+            sy[m] = partial_pair(ks[last], xs[m], 1 - mine, xs[m + 2], 1 - mine)
+            start(sy.at[m], ry.at[m], p_send.at[0], p_recv.at[m], device(x, beside, core, par))
+
+    def keep_pair():
+        for m in range(2):
+            sk[m] = partial_pair(ks[last], xs[m], mine, xs[m + 2], mine)
+
+    def spread_pair():
+        for m in (0, 1):
+            await_bytes(ry.at[m], p_recv.at[m])
+            qs[m] = (sk[m] + ry[m]).T
+            for d in ((2,), (1, 3))[m]:
+                start(
+                    qs.at[m, halves[d // 2]], xd.at[d - 1], d_send.at[0], d_recv.at[d - 1],
+                    device(xs[d], y, core, par),
+                )
+
+    main = range(last)
     if chunks == 4:
-        step_one(0)
-        step_one(1)
+        send_far(0)
+        send_far(1)
+        send_pair()
+        send_near(0)
+        send_far(2)
         step_two(0)
-        step_one(2)
+        send_near(1)
         step_two(1)
-        step_one(3)
-        for i in range(chunks):
+        send_near(2)
+        for i in main:
             own(i)
+        step_two(2)
+        keep_pair()
         finish(0)
-        step_two(2)
+        spread_pair()
         finish(1)
-        step_two(3)
         finish(2)
-        finish(3)
     else:
-        for i in range(chunks):
-            step_one(i)
-        for i in range(chunks):
+        send_pair()
+        for i in main:
+            send_far(i)
+            send_near(i)
+        for i in main:
             step_two(i)
             own(i)
-        for i in range(chunks):
+        keep_pair()
+        for i in main:
             finish(i)
+        spread_pair()
 
     mom_load.wait()
-    grads = ys[chunks - 1, pl.ds(pl.multiple_of(lax.rem(y, 2) * HALF, HALF), HALF), :]
-    for d in far_first:
-        await_bytes(yr.at[yy[d]], y_recv.at[yy[d]])
-        grads = grads + yr[yy[d]]
+    grads = qs[0, halves[0], :]
+    for i in main:
+        for j in range(2):
+            yv = 2 * ks[i] + j
+            await_bytes(yr.at[yv], y_recv.at[yv])
+            grads = grads + yr[yv]
+    for d in (1, 3, 2):
+        await_bytes(xd.at[d - 1], d_recv.at[d - 1])
+        grads = grads + xd[d - 1]
 
     grads_out[...] = grads
     blend = grads + retain * (retain * mv[...] + grads)
@@ -252,23 +292,53 @@
     total = jnp.sum(gram * identity, axis=(0, 1), keepdims=True)
     inverse = 1.0 / (jnp.sqrt(total) + epsilon)
 
+    def parts(a):
+        first_part = a.astype(jnp.bfloat16)
+        rest = a - first_part.astype(jnp.float32)
+        second_part = rest.astype(jnp.bfloat16)
+        third_part = (rest - second_part.astype(jnp.float32)).astype(jnp.bfloat16)
+        return first_part, second_part, third_part
+
     def dot(a, b):
-        return jnp.dot(a, b, precision=PRECISE, preferred_element_type=jnp.float32)
+        a1, a2, a3 = a
+        b1, b2, b3 = b
+        m = a1.shape[0]
+        upper = jnp.concatenate([a1, a2], axis=0)
+        high = jnp.dot(
+            jnp.concatenate([upper, upper], axis=1),
+            jnp.concatenate([b1, b2], axis=0),
+            preferred_element_type=jnp.float32,
+        )
+        low = jnp.dot(
+            jnp.concatenate([a1, a3], axis=1),
+            jnp.concatenate([b3, b1], axis=0),
+            preferred_element_type=jnp.float32,
+        )
+        return high[:m] + (high[m:] + low)
 
     state = blend * inverse
     gram = gram * (inverse * inverse)
     for step in range(ITERS):
-        square = dot(gram, gram)
-        poly = first_coef * identity + second_coef * gram + third_coef * square
-        state = dot(state, poly)
+        split = parts(gram)
+        square = dot(split, split)
+        poly = parts(first_coef * identity + second_coef * gram + third_coef * square)
         if step < ITERS - 1:
-            gram = dot(dot(gram, poly), poly)
+            both = [
+                jnp.concatenate([g, t], axis=0) for g, t in zip(split, parts(state))
+            ]
+            both = dot(both, poly)
+            state = both[HD:]
+            gram = dot(parts(both[:HD]), poly)
+        else:
+            state = dot(parts(state), poly)
     state_out[...] = state
 
     await_bytes(kv.at[pl.ds(1, 3)], key_sem.at[0])
     await_bytes(fr, f_send.at[0])
     await_bytes(rx, x_send.at[0])
-    await_bytes(yr.at[pl.ds(0, ny - 1)], y_send.at[0])
+    await_bytes(yr.at[pl.ds(0, ny - 2)], y_send.at[0])
+    await_bytes(ry, p_send.at[0])
+    await_bytes(xd, d_send.at[0])
     await_bytes(gr.at[pl.ds(0, 15)], g_send.at[0])
     await_bytes(hr.at[pl.ds(0, ny - 1)], g_send.at[1])
     await_bytes(ag.at[pl.ds(0, 15)], g_send.at[2])
@@ -277,6 +347,7 @@
 def on_device(features, key_partials, momentum):
     ny = lax.axis_size("fsdp") // (2 * NX)
     chunks = ny // 2
+    main = chunks - 1
     f32, bf16 = jnp.float32, jnp.bfloat16
     dma = pltpu.SemaphoreType.DMA
     block = jax.ShapeDtypeStruct((HALF, HD), f32)
@@ -299,13 +370,18 @@
             pltpu.VMEM((4, HD, HD), bf16),
             pltpu.VMEM((2 * HD, 2 * HD), bf16),
             pltpu.VMEM((HALF, HD), f32),
-            pltpu.VMEM((chunks, HD, HD), f32),
-            pltpu.VMEM((chunks, 2, HD, HD), f32),
-            pltpu.VMEM((chunks, HD, HD), f32),
-            pltpu.VMEM((3, chunks, 2, HALF, HD), f32),
-            pltpu.VMEM((chunks, 2, HALF, HD), f32),
-            pltpu.VMEM((chunks, HD, HD), f32),
+            pltpu.VMEM((main, HD, HD), f32),
+            pltpu.VMEM((main, 2, HD, HD), f32),
+            pltpu.VMEM((main, HD, HD), f32),
+            pltpu.VMEM((3, main, 2, HALF, HD), f32),
+            pltpu.VMEM((main, 2, HALF, HD), f32),
+            pltpu.VMEM((main, HD, HD), f32),
             pltpu.VMEM((ny, HALF, HD), f32),
+            pltpu.VMEM((2, HD, HD), f32),
+            pltpu.VMEM((2, HD, HD), f32),
+            pltpu.VMEM((2, HD, HD), f32),
+            pltpu.VMEM((2, HD, HD), f32),
+            pltpu.VMEM((NX - 1, HALF, HD), f32),
             pltpu.VMEM((HD, HD), f32),
             pltpu.VMEM((16, 8, HD), f32),
             pltpu.VMEM((ny, 8, HD), f32),
@@ -313,8 +389,10 @@
             dma((chunks + 2,)),
             dma((2,)),
             dma((1,)), dma((chunks,)),
-            dma((1,)), dma((3, chunks, 2)),
+            dma((1,)), dma((3, main, 2)),
             dma((1,)), dma((ny,)),
+            dma((1,)), dma((2,)),
+            dma((1,)), dma((NX - 1,)),
             dma((3,)), dma((3,)),
         ],
         compiler_params=pltpu.CompilerParams(

time: 53.6 us -> 51.4 us (0.959)
  Pallas kernels: 52.1 us -> 49.8 us
    pallas_call x1, Pallas kernels: 52.1 us -> 49.8 us  [on_device(): pl.pallas_call(body, name='muon_step', out_shape=(block, block), in_specs...]
where the time goes in v3:
time: 51.4 us; the launch traced here: 51.1 us
  Pallas kernels  49.8 us (97%)
  between operations  0.65 us (1%)
  other arithmetic  0.63 us (1%)
    pallas_call x1, Pallas kernels, on_device(): pl.pallas_call(body, name='muon_step', out_shape=(block, block), in_specs...  49.8 us

profile of v3, /device:TPU:1, one launch (start us, length us, event | category | flops | bytes accessed | tf_op | source)
XLA Modules:
  0.0 51.1 jit_solution(4028518445429045042)
XLA Ops:
  0.6 0.0 copy-start
  0.6 49.8 %muon_step.1 = (f32[64,128]{1,0:T(8,128)S(1)}, f32[64,128]{1,0:T(8,128)S(1)}) custom-call(bf16[128,8192]{1,0:T(8,128)(2,1)} %refs_0_.1, bf16[128,128]{1,0:T(8,128)(2,1)} %bitcast.10, f32[64,128]{1,0:T(8,128)} %bitcast.8), custom_call_target="tpu_custom_call" | custom-call | tf_op jit(solution)/shard_map/muon_step/pallas_call | solution.py:361
  50.5 0.0 copy-done
  50.5 0.6 %multiply_add_fusion = (f32[64,128]{1,0:T(8,128)}, f32[64,128]{1,0:T(8,128)}) fusion(f32[64,128]{1,0:T(8,128)S(1)} %get-tuple-element.5, f32[64,128]{1,0:T(8,128)S(1)} %bitcast.9, f32[64,128]{1,0:T(8,128)S(1)} %get-tuple-element.4), kind=kLoop, calls=%fused_computation | loop fusion | flops 24576 | bytes 163840 | tf_op jit(solution)/shard_map/add | solution.py:403
Async XLA Ops:
  0.6 49.9 %copy-start = (f32[64,1,128]{2,1,0:T(1,128)S(1)}, f32[64,1,128]{2,1,0:T(1,128)}, u32[]{:S(2)}) copy-start(f32[64,1,128]{2,1,0:T(1,128)} %param.5) | copy-start | bytes 98308

commit v4 on v3

--- a/solution.py
+++ b/solution.py
@@ -108,8 +108,10 @@
     key_load.wait()
     pl.semaphore_wait(barrier, 15 + ny - 1)
 
-    for cc, pp, slot in ((cs[1], ps[1], 3), (core, ps[1], 2), (cs[1], par, 1)):
-        start(kv.at[0], kv.at[slot], key_sem.at[0], key_sem.at[1], device(x, y, cc, pp))
+    for cc in range(2):
+        apart = (core + cc) - 2 * core * cc
+        start(kv.at[0], kv.at[2 + apart], key_sem.at[0], key_sem.at[1], device(x, y, cc, ps[1]))
+    start(kv.at[0], kv.at[1], key_sem.at[0], key_sem.at[1], device(x, y, cs[1], par))
     for i in range(chunks):
         await_bytes(fv.at[ks[i]], load_sem.at[i])
         for xx in (2, 1, 3, 0):
@@ -151,18 +153,22 @@
     near = (x + 1 - 2 * lax.rem(x, 2), 3 - x)
     halves = (pl.ds(0, HALF), pl.ds(HALF, HALF))
 
-    def send_far(i):
+    def compute_far(i):
         await_bytes(fr.at[ks[i]], f_recv.at[i])
         sf[i] = partial_for(ks[i], xs[2])
+
+    def send_far(i):
         for h in range(2):
             start(
                 sf.at[i, halves[h]], rx.at[0, i, h], x_send.at[0], x_recv.at[0, i, h],
                 device(near[h], y, core, par),
             )
 
-    def send_near(i):
+    def compute_near(i):
         for a in range(2):
             pn[i, a] = partial_for(ks[i], near[a])
+
+    def send_near(i):
         for h in range(2):
             start(
                 pn.at[i, h, halves[h]], rx.at[1, i, h], x_send.at[0], x_recv.at[1, i, h],
@@ -195,10 +201,13 @@
     beside = 2 * ky + 1 - mine
     last = chunks - 1
 
-    def send_pair():
+    def compute_pair():
         await_bytes(fr.at[ks[last]], f_recv.at[last])
         for m in range(2):
             sy[m] = partial_pair(ks[last], xs[m], 1 - mine, xs[m + 2], 1 - mine)
+
+    def send_pair():
+        for m in range(2):
             start(sy.at[m], ry.at[m], p_send.at[0], p_recv.at[m], device(x, beside, core, par))
 
     def keep_pair():
@@ -216,36 +225,30 @@
                 )
 
     main = range(last)
-    if chunks == 4:
-        send_far(0)
-        send_far(1)
-        send_pair()
-        send_near(0)
-        send_far(2)
-        step_two(0)
-        send_near(1)
-        step_two(1)
-        send_near(2)
-        for i in main:
-            own(i)
-        step_two(2)
-        keep_pair()
-        finish(0)
-        spread_pair()
-        finish(1)
-        finish(2)
-    else:
-        send_pair()
-        for i in main:
-            send_far(i)
-            send_near(i)
-        for i in main:
-            step_two(i)
-            own(i)
-        keep_pair()
-        for i in main:
-            finish(i)
-        spread_pair()
+    compute_far(0)
+    send_far(0)
+    compute_near(0)
+    send_near(0)
+    for i in main[1:]:
+        compute_far(i)
+    for i in main[1:]:
+        send_far(i)
+    compute_pair()
+    send_pair()
+    step_two(0)
+    for i in main[1:]:
+        compute_near(i)
+        send_near(i)
+    for i in main[1:]:
+        step_two(i)
+    own(0)
+    keep_pair()
+    finish(0)
+    spread_pair()
+    for i in main[1:]:
+        own(i)
+    for i in main[1:]:
+        finish(i)
 
     mom_load.wait()
     grads = qs[0, halves[0], :]
@@ -263,28 +266,32 @@
     contract = (((0,), (0,)), ((), ()))
     gs[...] = lax.dot_general(
         blend, blend, contract, precision=PRECISE, preferred_element_type=jnp.float32
-    )
-
-    def piece(b):
-        return pl.ds(pl.multiple_of(b * 8, 8), 8)
-
-    for xx, cc, pp in others:
+    ).reshape(8, 16, HD)
+
+    owner = x * 2 + par
+    owners = [(xs[dx], ps[dp]) for dx in (2, 1, 3, 0) for dp in (1, 0)]
+    for xx, pp in owners[:-1]:
         start(
-            gs.at[piece(number(xx, cc, pp))], gr.at[member], g_send.at[0], g_recv.at[0],
-            device(xx, y, cc, pp),
+            gs.at[xx * 2 + pp], gr.at[member], g_send.at[0], g_recv.at[0], device(xx, y, 1, pp)
         )
-    gr[member] = gs[piece(member), :]
-    await_bytes(gr.at[pl.ds(0, 15)], g_recv.at[0])
-    hr[y] = jnp.sum(gr[...], axis=0)
-    for d in far_first:
-        start(hr.at[y], hr.at[y], g_send.at[1], g_recv.at[1], device(x, yy[d], core, par))
-    await_bytes(hr.at[pl.ds(0, ny - 1)], g_recv.at[1])
-    ag[member] = jnp.sum(hr[...], axis=0)
-    for xx, cc, pp in others:
-        start(
-            ag.at[member], ag.at[member], g_send.at[2], g_recv.at[2], device(xx, y, cc, pp)
-        )
-    await_bytes(ag.at[pl.ds(0, 15)], g_recv.at[2])
+
+    @pl.when(core == 0)
+    def _():
+        start(gs.at[owner], gr.at[member], g_send.at[0], g_recv.at[0], device(x, y, 1, par))
+        await_bytes(ag, g_recv.at[2])
+
+    @pl.when(core == 1)
+    def _():
+        gr[member] = gs[owner]
+        await_bytes(gr.at[pl.ds(0, 15)], g_recv.at[0])
+        hr[y] = jnp.sum(gr[...], axis=0)
+        for d in far_first:
+            start(hr.at[y], hr.at[y], g_send.at[1], g_recv.at[1], device(x, yy[d], 1, par))
+        await_bytes(hr.at[pl.ds(0, ny - 1)], g_recv.at[1])
+        ag[owner] = jnp.sum(hr[...], axis=0)
+        for xx, cc, pp in others:
+            start(ag.at[owner], ag.at[owner], g_send.at[2], g_recv.at[2], device(xx, y, cc, pp))
+        await_bytes(ag.at[pl.ds(0, 7)], g_recv.at[2])
 
     gram = ag[...].reshape(HD, HD)
     row = lax.broadcasted_iota(jnp.int32, (HD, HD), 0)
@@ -339,9 +346,16 @@
     await_bytes(yr.at[pl.ds(0, ny - 2)], y_send.at[0])
     await_bytes(ry, p_send.at[0])
     await_bytes(xd, d_send.at[0])
-    await_bytes(gr.at[pl.ds(0, 15)], g_send.at[0])
-    await_bytes(hr.at[pl.ds(0, ny - 1)], g_send.at[1])
-    await_bytes(ag.at[pl.ds(0, 15)], g_send.at[2])
+    await_bytes(gs.at[pl.ds(0, 7)], g_send.at[0])
+
+    @pl.when(core == 0)
+    def _():
+        await_bytes(gs.at[0], g_send.at[0])
+
+    @pl.when(core == 1)
+    def _():
+        await_bytes(hr.at[pl.ds(0, ny - 1)], g_send.at[1])
+        await_bytes(gr.at[pl.ds(0, 15)], g_send.at[2])
 
 
 def on_device(features, key_partials, momentum):
@@ -382,10 +396,10 @@
             pltpu.VMEM((2, HD, HD), f32),
             pltpu.VMEM((2, HD, HD), f32),
             pltpu.VMEM((NX - 1, HALF, HD), f32),
-            pltpu.VMEM((HD, HD), f32),
-            pltpu.VMEM((16, 8, HD), f32),
-            pltpu.VMEM((ny, 8, HD), f32),
-            pltpu.VMEM((16, 8, HD), f32),
+            pltpu.VMEM((8, 16, HD), f32),
+            pltpu.VMEM((16, 16, HD), f32),
+            pltpu.VMEM((ny, 16, HD), f32),
+            pltpu.VMEM((8, 16, HD), f32),
             dma((chunks + 2,)),
             dma((2,)),
             dma((1,)), dma((chunks,)),

time: 51.4 us -> 49.6 us (0.965)
  Pallas kernels: 49.8 us -> 48.1 us
    pallas_call x1, Pallas kernels: 49.8 us -> 48.1 us  [on_device(): pl.pallas_call(body, name='muon_step', out_shape=(block, block), in_specs...]
where the time goes in v4:
time: 49.6 us; the launch traced here: 49.4 us
  Pallas kernels  48.1 us (97%)
  between operations  0.65 us (1%)
  other arithmetic  0.63 us (1%)
    pallas_call x1, Pallas kernels, on_device(): pl.pallas_call(body, name='muon_step', out_shape=(block, block), in_specs...  48.1 us

profile of v4, /device:TPU:1, one launch (start us, length us, event | category | flops | bytes accessed | tf_op | source)
XLA Modules:
  0.0 49.4 jit_solution(12254924505449328114)
XLA Ops:
  0.6 0.0 copy-start
  0.6 48.1 %muon_step.1 = (f32[64,128]{1,0:T(8,128)S(1)}, f32[64,128]{1,0:T(8,128)S(1)}) custom-call(bf16[128,8192]{1,0:T(8,128)(2,1)} %refs_0_.1, bf16[128,128]{1,0:T(8,128)(2,1)} %bitcast.10, f32[64,128]{1,0:T(8,128)} %bitcast.8), custom_call_target="tpu_custom_call" | custom-call | tf_op jit(solution)/shard_map/muon_step/pallas_call | solution.py:375
  48.8 0.0 copy-done
  48.8 0.6 %multiply_add_fusion = (f32[64,128]{1,0:T(8,128)}, f32[64,128]{1,0:T(8,128)}) fusion(f32[64,128]{1,0:T(8,128)S(1)} %get-tuple-element.5, f32[64,128]{1,0:T(8,128)S(1)} %bitcast.9, f32[64,128]{1,0:T(8,128)S(1)} %get-tuple-element.4), kind=kLoop, calls=%fused_computation | loop fusion | flops 24576 | bytes 163840 | tf_op jit(solution)/shard_map/add | solution.py:417
Async XLA Ops:
  0.6 48.1 %copy-start = (f32[64,1,128]{2,1,0:T(1,128)S(1)}, f32[64,1,128]{2,1,0:T(1,128)}, u32[]{:S(2)}) copy-start(f32[64,1,128]{2,1,0:T(1,128)} %param.5) | copy-start | bytes 98308

commit v5 on v4

--- a/solution.py
+++ b/solution.py
@@ -31,7 +31,7 @@
 def step_kernel(
     ny, feat, keys, mom, state_out, grads_out,
     fv, fr, kv, lhs, mv, sf, pn, px, rx, fw, ys, yr, sy, ry, sk, qs, xd, gs, gr, hr, ag,
-    load_sem, key_sem, f_send, f_recv, x_send, x_recv, y_send, y_recv, p_send, p_recv, d_send, d_recv,
+    load_sem, key_sem, f_send, f_recv, x_send, x_recv, far_recv, y_send, y_recv, p_send, p_recv, d_send, d_recv,
     g_send, g_recv,
 ):
     chunks = ny // 2
@@ -44,6 +44,7 @@
     x = lax.div(chip, ny)
     par = lax.rem(z, 2)
     ky = lax.div(y, 2)
+    mine = lax.rem(y, 2)
     zpair = z - par
 
     xs = [x] + [lax.rem(x + d, NX) for d in range(1, NX)]
@@ -160,7 +161,7 @@
     def send_far(i):
         for h in range(2):
             start(
-                sf.at[i, halves[h]], rx.at[0, i, h], x_send.at[0], x_recv.at[0, i, h],
+                sf.at[i, halves[h]], rx.at[0, i, h], x_send.at[0], far_recv.at[i, h],
                 device(near[h], y, core, par),
             )
 
@@ -171,16 +172,16 @@
     def send_near(i):
         for h in range(2):
             start(
-                pn.at[i, h, halves[h]], rx.at[1, i, h], x_send.at[0], x_recv.at[1, i, h],
+                pn.at[i, h, halves[h]], rx.at[1, i, h], x_send.at[0], x_recv.at[i],
                 device(near[h], y, core, par),
             )
 
     def step_two(i):
         for h in range(2):
-            await_bytes(rx.at[0, i, h], x_recv.at[0, i, h])
+            await_bytes(rx.at[0, i, h], far_recv.at[i, h])
             fw[i, h] = pn[i, 1 - h, halves[h], :] + rx[0, i, h]
             start(
-                fw.at[i, h], rx.at[2, i, h], x_send.at[0], x_recv.at[2, i, h],
+                fw.at[i, h], rx.at[2, i, h], x_send.at[0], x_recv.at[i],
                 device(near[1 - h], y, core, par),
             )
 
@@ -188,16 +189,17 @@
         px[i] = partial_for(ks[i], x)
 
     def finish(i):
-        for stage in (1, 2):
-            for h in range(2):
-                await_bytes(rx.at[stage, i, h], x_recv.at[stage, i, h])
+        await_bytes(ry, x_recv.at[i])
         total = px[i] + (rx[1, i] + rx[2, i]).reshape(HD, HD)
         ys[i] = total.T
-        for j in range(2):
-            yv = 2 * ks[i] + j
-            start(ys.at[i, halves[j]], yr.at[y], y_send.at[0], y_recv.at[y], device(x, yv, core, par))
-
-    mine = lax.rem(y, 2)
+        farther = {0: 0, 1: 1, 2: mine, 3: 0}[order[i]]
+        for j in (farther, 1 - farther):
+            rows = pl.ds(pl.multiple_of(j * HALF, HALF), HALF)
+            start(
+                ys.at[i, rows], yr.at[y], y_send.at[0], y_recv.at[0],
+                device(x, 2 * ks[i] + j, core, par),
+            )
+
     beside = 2 * ky + 1 - mine
     last = chunks - 1
 
@@ -220,7 +222,7 @@
             qs[m] = (sk[m] + ry[m]).T
             for d in ((2,), (1, 3))[m]:
                 start(
-                    qs.at[m, halves[d // 2]], xd.at[d - 1], d_send.at[0], d_recv.at[d - 1],
+                    qs.at[m, halves[d // 2]], xd.at[d - 1], d_send.at[0], d_recv.at[0],
                     device(xs[d], y, core, par),
                 )
 
@@ -241,8 +243,8 @@
         send_near(i)
     for i in main[1:]:
         step_two(i)
+    keep_pair()
     own(0)
-    keep_pair()
     finish(0)
     spread_pair()
     for i in main[1:]:
@@ -252,14 +254,13 @@
 
     mom_load.wait()
     grads = qs[0, halves[0], :]
+    await_bytes(xd, d_recv.at[0])
+    for d in (1, 2, 3):
+        grads = grads + xd[d - 1]
+    await_bytes(yr.at[pl.ds(0, ny - 2)], y_recv.at[0])
     for i in main:
         for j in range(2):
-            yv = 2 * ks[i] + j
-            await_bytes(yr.at[yv], y_recv.at[yv])
-            grads = grads + yr[yv]
-    for d in (1, 3, 2):
-        await_bytes(xd.at[d - 1], d_recv.at[d - 1])
-        grads = grads + xd[d - 1]
+            grads = grads + yr[2 * ks[i] + j]
 
     grads_out[...] = grads
     blend = grads + retain * (retain * mv[...] + grads)
@@ -403,10 +404,10 @@
             dma((chunks + 2,)),
             dma((2,)),
             dma((1,)), dma((chunks,)),
-            dma((1,)), dma((3, main, 2)),
-            dma((1,)), dma((ny,)),
+            dma((1,)), dma((main,)), dma((main, 2)),
+            dma((1,)), dma((1,)),
             dma((1,)), dma((2,)),
-            dma((1,)), dma((NX - 1,)),
+            dma((1,)), dma((1,)),
             dma((3,)), dma((3,)),
         ],
         compiler_params=pltpu.CompilerParams(

time: 49.6 us -> 49.5 us (level)
  no operation moved by 1% of the time
where the time goes in v5:
time: 49.5 us; the launch traced here: 49.2 us
  Pallas kernels  48 us (97%)
  between operations  0.65 us (1%)
  other arithmetic  0.63 us (1%)
    pallas_call x1, Pallas kernels, on_device(): pl.pallas_call(body, name='muon_step', out_shape=(block, block), in_specs...  48 us

profile of v5, /device:TPU:1, one launch (start us, length us, event | category | flops | bytes accessed | tf_op | source)
XLA Modules:
  0.0 49.2 jit_solution(17650232319034751390)
XLA Ops:
  0.6 0.0 copy-start
  0.6 48.0 %muon_step.1 = (f32[64,128]{1,0:T(8,128)S(1)}, f32[64,128]{1,0:T(8,128)S(1)}) custom-call(bf16[128,8192]{1,0:T(8,128)(2,1)} %refs_0_.1, bf16[128,128]{1,0:T(8,128)(2,1)} %bitcast.10, f32[64,128]{1,0:T(8,128)} %bitcast.8), custom_call_target="tpu_custom_call" | custom-call | tf_op jit(solution)/shard_map/muon_step/pallas_call | solution.py:376
  48.6 0.0 copy-done
  48.6 0.6 %multiply_add_fusion = (f32[64,128]{1,0:T(8,128)}, f32[64,128]{1,0:T(8,128)}) fusion(f32[64,128]{1,0:T(8,128)S(1)} %get-tuple-element.5, f32[64,128]{1,0:T(8,128)S(1)} %bitcast.9, f32[64,128]{1,0:T(8,128)S(1)} %get-tuple-element.4), kind=kLoop, calls=%fused_computation | loop fusion | flops 24576 | bytes 163840 | tf_op jit(solution)/shard_map/add | solution.py:418
Async XLA Ops:
  0.6 48.0 %copy-start = (f32[64,1,128]{2,1,0:T(1,128)S(1)}, f32[64,1,128]{2,1,0:T(1,128)}, u32[]{:S(2)}) copy-start(f32[64,1,128]{2,1,0:T(1,128)} %param.5) | copy-start | bytes 98308

commit v6 on v5

--- a/solution.py
+++ b/solution.py
@@ -112,7 +112,7 @@
     for cc in range(2):
         apart = (core + cc) - 2 * core * cc
         start(kv.at[0], kv.at[2 + apart], key_sem.at[0], key_sem.at[1], device(x, y, cc, ps[1]))
-    start(kv.at[0], kv.at[1], key_sem.at[0], key_sem.at[1], device(x, y, cs[1], par))
+    start(kv.at[0], kv.at[1], key_sem.at[0], key_sem.at[2], device(x, y, cs[1], par))
     for i in range(chunks):
         await_bytes(fv.at[ks[i]], load_sem.at[i])
         for xx in (2, 1, 3, 0):
@@ -126,8 +126,10 @@
                     device(x, y, 1 - core, par),
                 )
 
-    await_bytes(kv.at[pl.ds(1, 3)], key_sem.at[1])
+    await_bytes(kv.at[1], key_sem.at[2])
     for r in range(2):
+        if r == 1:
+            await_bytes(kv.at[pl.ds(2, 2)], key_sem.at[1])
         for f in range(2):
             lhs[r * HD : (r + 1) * HD, f * HD : (f + 1) * HD] = kv[2 * r + f].T
 
@@ -402,7 +404,7 @@
             pltpu.VMEM((ny, 16, HD), f32),
             pltpu.VMEM((8, 16, HD), f32),
             dma((chunks + 2,)),
-            dma((2,)),
+            dma((3,)),
             dma((1,)), dma((chunks,)),
             dma((1,)), dma((main,)), dma((main, 2)),
             dma((1,)), dma((1,)),

time: 49.5 us -> 49.5 us (level)
  no operation moved by 1% of the time
where the time goes in v6:
time: 49.5 us; the launch traced here: 49.2 us
  Pallas kernels  47.9 us (97%)
  between operations  0.65 us (1%)
  other arithmetic  0.63 us (1%)
    pallas_call x1, Pallas kernels, on_device(): pl.pallas_call(body, name='muon_step', out_shape=(block, block), in_specs...  47.9 us

profile of v6, /device:TPU:1, one launch (start us, length us, event | category | flops | bytes accessed | tf_op | source)
XLA Modules:
  0.0 49.2 jit_solution(7759508424980881758)
XLA Ops:
  0.6 0.0 copy-start
  0.6 47.9 %muon_step.1 = (f32[64,128]{1,0:T(8,128)S(1)}, f32[64,128]{1,0:T(8,128)S(1)}) custom-call(bf16[128,8192]{1,0:T(8,128)(2,1)} %refs_0_.1, bf16[128,128]{1,0:T(8,128)(2,1)} %bitcast.10, f32[64,128]{1,0:T(8,128)} %bitcast.8), custom_call_target="tpu_custom_call" | custom-call | tf_op jit(solution)/shard_map/muon_step/pallas_call | solution.py:378
  48.6 0.0 copy-done
  48.6 0.6 %multiply_add_fusion = (f32[64,128]{1,0:T(8,128)}, f32[64,128]{1,0:T(8,128)}) fusion(f32[64,128]{1,0:T(8,128)S(1)} %get-tuple-element.5, f32[64,128]{1,0:T(8,128)S(1)} %bitcast.9, f32[64,128]{1,0:T(8,128)S(1)} %get-tuple-element.4), kind=kLoop, calls=%fused_computation | loop fusion | flops 24576 | bytes 163840 | tf_op jit(solution)/shard_map/add | solution.py:420
Async XLA Ops:
  0.6 48.0 %copy-start = (f32[64,1,128]{2,1,0:T(1,128)S(1)}, f32[64,1,128]{2,1,0:T(1,128)}, u32[]{:S(2)}) copy-start(f32[64,1,128]{2,1,0:T(1,128)} %param.5) | copy-start | bytes 98308
